TPU v7x, 32 devices: a whole 2x2x4 slice. The times are simulated.
32 devices in a mesh: grp: 2 (over y), tm: 16 (over z, x, core).
Axes of the slice: x: 2, y: 2, z: 4, core: 2. Of those that a mesh axis runs over, the one named last changes fastest.
Arguments:
- traces: float32 [2048, 16384], P('grp', 'tm'), parts along dimension 0, may hold values from -6 to 6
- templates: float32 [64, 8192], P('tm'), may hold values from -6 to 6
- moveouts: int32 [2048], P('grp'), parts along dimension 0, may hold values from 0 to 2047
- masks: int32 [64, 2048], P(None, 'grp'), parts along dimension 1, may hold values 0 or 1
Outputs:
- detection: float32 [64, 16384], P('tm', 'grp'), parts along dimension 1
There are 2 independent parts, one for each index of `grp`. A program takes and returns all parts, laid end to end along the dimension named above; an argument that names none is the same for every part. Nothing has to cross between parts.
All inputs are finite; a program needn't handle non-finite values.
Results may differ from a plain program's by a relative error of at most 0.000073.
Values sent between devices are 32-bit elements; how exact they have to be, the bound alone decides.
A program may use at most 64 MiB of HBM per device.

v0:
```python
import functools
import math

import jax
import jax.numpy as jnp
import numpy as np
from jax import lax
from jax.experimental import pallas as pl
from jax.experimental.pallas import tpu as pltpu
from jax.sharding import PartitionSpec as P

f32, bf16 = jnp.float32, jnp.bfloat16
LANES = 128
REACH = 2048
COARSE = 4


def split(value):
    high = value.astype(bf16)
    return high, (value - high.astype(f32)).astype(bf16)


def split_table(table):
    high = table.astype(jnp.bfloat16)
    return high, (table - high.astype(np.float64)).astype(jnp.bfloat16)


def transform(rows, first_ref, forward_ref, cosine, sine):
    outer = cosine.shape[0]
    high, low = split(jnp.concatenate(rows, axis=1))
    first = jnp.dot(first_ref[...], jnp.concatenate([high, high, low], axis=0), preferred_element_type=f32)
    turned = []
    for r in range(len(rows)):
        re = first[:outer, r * LANES : (r + 1) * LANES]
        im = first[outer:, r * LANES : (r + 1) * LANES]
        turned.append(jnp.concatenate([re * cosine + im * sine, im * cosine - re * sine], axis=1))
    high, low = split(jnp.concatenate(turned, axis=0))
    return jnp.dot(jnp.concatenate([high, low, high], axis=1), forward_ref[...], preferred_element_type=f32)


def shift(traces_ref, late, terms, base, group, channels):
    rows = 16
    blocks = traces_ref.shape[1] // LANES
    here = pl.ds(pl.multiple_of(group * rows, rows), rows)
    delay = late[here, :]
    lane = lax.broadcasted_iota(jnp.int32, (rows, LANES), 1)
    inner = (delay & (LANES - 1)) + 1
    index = (lane - inner) & (LANES - 1)
    keep = lane >= inner
    turned = [
        jnp.take_along_axis(
            traces_ref[here, b * LANES : (b + 1) * LANES], index, axis=1, mode="promise_in_bounds"
        )
        for b in range(blocks)
    ]
    zero = jnp.zeros((rows, LANES), f32)
    moved = [
        jnp.where(keep, turned[b] if b < blocks else zero, turned[b - 1] if b > 0 else zero)
        for b in range(blocks + 1)
    ]
    hop = 1
    while hop < COARSE:
        chosen = ((delay // LANES) & hop) != 0
        moved = [
            jnp.where(
                chosen,
                moved[b - hop] if b >= hop else zero,
                moved[b] if b < len(moved) else zero,
            )
            for b in range(len(moved) + hop)
        ]
        hop *= 2
    for b in range(len(moved)):
        high, low = split(moved[b])
        column = slice(b * LANES, (b + 1) * LANES)
        terms[pl.ds(pl.multiple_of(base + group * rows, rows), rows), column] = high
        terms[pl.ds(pl.multiple_of(channels + base + group * rows, rows), rows), column] = low


def kernel(
    devices,
    channels,
    moveout_ref,
    moveouts_ref,
    traces_ref,
    mask_hbm,
    template_hbm,
    first_hbm,
    forward_hbm,
    back_hbm,
    last_hbm,
    twiddle_hbm,
    out_ref,
    mask_ref,
    template_ref,
    first_ref,
    forward_ref,
    back_ref,
    last_ref,
    twiddle_ref,
    late,
    terms,
    raw,
    part,
    arrived,
    merged,
    joined,
    series,
    tail,
    load_sem,
    pair_send,
    pair_recv,
    send_sem,
    recv_sem,
):
    step = pl.program_id(0)
    steps = pl.num_programs(0)
    depth, width = traces_ref.shape
    each, lags = template_ref.shape
    pairs = devices // 2
    me = lax.axis_index("tm")
    core = lax.rem(me, 2)
    pair = me // 2
    partner = me + 1 - 2 * core
    blocks = width // LANES
    window = blocks + REACH // LANES
    outer = devices * blocks
    loads = [
        pltpu.make_async_copy(source, target, load_sem.at[i])
        for i, (source, target) in enumerate(
            (
                (mask_hbm, mask_ref),
                (template_hbm, template_ref),
                (first_hbm, first_ref),
                (forward_hbm, forward_ref),
                (twiddle_hbm, twiddle_ref),
                (back_hbm, back_ref),
                (last_hbm, last_ref),
            )
        )
    ]
    barrier = pltpu.get_barrier_semaphore()

    @pl.when(step == 0)
    def _():
        for load in loads:
            load.start()

        def greet(i, _):
            target = 2 * lax.rem(pair + i, pairs) + core
            pl.semaphore_signal(barrier, inc=1, device_id={"tm": target}, device_id_type=pl.DeviceIdType.MESH)
            return 0

        pl.semaphore_signal(barrier, inc=1, device_id={"tm": partner}, device_id_type=pl.DeviceIdType.MESH)
        lax.fori_loop(1, pairs, greet, 0)

    for piece in range(depth // LANES):
        row = (REACH - 1) - moveout_ref[:, piece * LANES : (piece + 1) * LANES]
        late[piece * LANES : (piece + 1) * LANES, :] = jnp.broadcast_to(row, (LANES, LANES)).T

    def four_groups(i, _):
        for k in range(4):
            shift(traces_ref, late, terms, step * depth, 4 * i + k, channels)
        return 0

    lax.fori_loop(0, depth // 64, four_groups, 0)

    def peer(k):
        return lax.rem(pair + 1 + k, pairs)

    def to_partner(g):
        return pltpu.make_async_remote_copy(
            src_ref=part.at[1 - core, g],
            dst_ref=arrived.at[g],
            send_sem=pair_send.at[g],
            recv_sem=pair_recv.at[g],
            device_id={"tm": partner},
            device_id_type=pl.DeviceIdType.MESH,
        )

    def to_owner(k):
        g = peer(k)
        return pltpu.make_async_remote_copy(
            src_ref=merged.at[g],
            dst_ref=joined.at[pair],
            send_sem=send_sem.at[k],
            recv_sem=recv_sem.at[k],
            device_id={"tm": 2 * g + core},
            device_id_type=pl.DeviceIdType.MESH,
        )

    @pl.when(step == steps - 1)
    def _():
        loads[0].wait()
        count = mask_ref.shape[0]
        coarse = ((REACH - 1) - moveouts_ref[...]) // (COARSE * LANES)
        chosen = [
            jnp.where(coarse == h, mask_ref[...], 0).astype(f32).astype(bf16)
            for h in range(REACH // LANES // COARSE)
        ]
        masks = jnp.concatenate(chosen, axis=0)
        double = jnp.concatenate([masks, masks], axis=1)
        fine = blocks + COARSE
        span = 2 if fine % 2 == 0 else 1
        for b in range(0, fine, span):
            column = slice(b * LANES, (b + span) * LANES)
            raw[:, column] = jnp.dot(double, terms[:, column], preferred_element_type=f32)

        def stacked(b):
            hops = [h for h in range(len(chosen)) if 0 <= b - COARSE * h < fine]
            return sum(
                raw[h * count : (h + 1) * count, (b - COARSE * h) * LANES : (b - COARSE * h + 1) * LANES]
                for h in hops
            )

        span = 2 if window % 2 == 0 else 1
        for b in range(0, window, span):
            added = [stacked(b + j) for j in range(span)]
            for owner in range(devices):
                part[owner % 2, owner // 2, b * each : (b + span) * each, :] = jnp.concatenate(
                    [value[owner * each : (owner + 1) * each] for value in added], axis=0
                )
        pl.semaphore_wait(barrier, pairs)

        def first_send(k, _):
            to_partner(peer(k)).start()
            return 0

        lax.fori_loop(0, pairs - 1, first_send, 0)
        to_partner(pair).start()
        rows, more = window * each, blocks * each

        def merge(g):
            to_partner(g).wait_recv()
            own, other = part[core, g], arrived[g]
            early = jnp.where(core == 0, own, other)
            later = jnp.where(core == 0, other, own)
            middle = early[more:] + later[: rows - more]
            return early[:more], middle, later[rows - more :]

        def second_send(k, _):
            g = peer(k)
            begin, middle, end = merge(g)
            merged[g, 0:more] = begin
            merged[g, more:rows] = middle
            merged[g, rows : rows + more] = end
            to_owner(k).start()
            return 0

        lax.fori_loop(0, pairs - 1, second_send, 0)
        begin, middle, end = merge(pair)
        joined[pair, 0:more] = begin
        joined[pair, more:rows] = middle
        joined[pair, rows : rows + more] = end

        for load in loads[1:]:
            load.wait()
        cosine, sine = twiddle_ref[0], twiddle_ref[1]
        values = template_ref[...]
        count = lags // LANES
        for b in range(count):
            series[b * each : (b + 1) * each, :] = values[:, b * LANES : (b + 1) * LANES]
        series[count * each :, :] = jnp.zeros(((outer - count) * each, LANES), f32)
        energy = jnp.sqrt(jnp.sum(values * values, axis=1, keepdims=True) + 1e-06)
        factor = 1.0 / (outer * LANES * math.sqrt(channels) * energy)

        def columns():
            return [series[pl.ds(k, outer, stride=each), :] for k in range(each)]

        templ = transform(columns(), first_ref, forward_ref, cosine, sine)

        def finish(k, _):
            to_owner(k).wait()
            return 0

        lax.fori_loop(0, pairs - 1, finish, 0)

        def leave(g, _):
            to_partner(g).wait_send()
            return 0

        lax.fori_loop(0, pairs, leave, 0)
        series[...] = jnp.zeros(series.shape, f32)
        local = 2 * blocks
        wide = window + blocks
        for source in range(pairs):
            for b in range(0, wide, local):
                taken = min(local, wide - b)
                block = (source * local + b - REACH // LANES) % outer
                here = slice(block * each, (block + taken) * each)
                series[here, :] = series[here, :] + joined[source, b * each : (b + taken) * each, :]
        stack = transform(columns(), first_ref, forward_ref, cosine, sine)
        stack_re, stack_im = stack[:, :LANES], stack[:, LANES:]
        templ_re, templ_im = templ[:, :LANES], templ[:, LANES:]
        product = jnp.concatenate(
            [stack_re * templ_re + stack_im * templ_im, stack_im * templ_re - stack_re * templ_im], axis=1
        )
        high, low = split(product)
        back = jnp.dot(jnp.concatenate([high, low, high], axis=1), back_ref[...], preferred_element_type=f32)
        turned = []
        for k in range(each):
            re = back[k * outer : (k + 1) * outer, :LANES]
            im = back[k * outer : (k + 1) * outer, LANES:]
            turned.append(jnp.concatenate([re * cosine - im * sine, re * sine + im * cosine], axis=0))
        high, low = split(jnp.concatenate(turned, axis=1))
        final = jnp.dot(last_ref[...], jnp.concatenate([high, high, low], axis=0), preferred_element_type=f32)
        for k in range(each):
            tail[pl.ds(k, count, stride=each), :] = final[:, k * LANES : (k + 1) * LANES]
        for b in range(count):
            out_ref[:, b * LANES : (b + 1) * LANES] = tail[b * each : (b + 1) * each, :] * factor


def tables(length, lags):
    outer = length // LANES
    turn = 2.0 * math.pi
    ramp = np.arange(outer)[:, None] * np.arange(outer)[None, :] % outer * (turn / outer)
    wide = np.arange(LANES)[:, None] * np.arange(LANES)[None, :] % LANES * (turn / LANES)
    twist = np.arange(outer)[:, None] * np.arange(LANES)[None, :] % length * (turn / length)
    first = split_table(np.concatenate([np.cos(ramp), -np.sin(ramp)], axis=0))
    cosine, sine = np.cos(wide), np.sin(wide)
    forward = split_table(np.block([[cosine, -sine], [sine, cosine]]))
    back = split_table(np.block([[cosine, sine], [-sine, cosine]]))
    shown = ramp[: lags // LANES]
    last = split_table(np.concatenate([np.cos(shown), -np.sin(shown)], axis=1))
    return (
        np.concatenate([first[0], first[1], first[0]], axis=1),
        np.concatenate([forward[0], forward[0], forward[1]], axis=0),
        np.concatenate([back[0], back[0], back[1]], axis=0),
        np.concatenate([last[0], last[1], last[0]], axis=1),
        np.stack([np.cos(twist), np.sin(twist)]).astype(np.float32),
    )


def on_device(devices, traces, templates, moveouts, masks):
    channels, width = traces.shape
    each, lags = templates.shape
    blocks = width // LANES
    outer = devices * blocks
    window = blocks + REACH // LANES
    depth = math.gcd(channels, 256)
    pairs = devices // 2
    loaded = [masks, templates, *[jnp.asarray(table) for table in tables(outer * LANES, lags)]]
    wide = (window + blocks) * each
    return pl.pallas_call(
        functools.partial(kernel, devices, channels),
        grid=(channels // depth,),
        in_specs=[
            pl.BlockSpec((1, depth), lambda i: (0, i)),
            pl.BlockSpec((1, channels), lambda i: (0, 0)),
            pl.BlockSpec((depth, width), lambda i: (i, 0)),
            *[pl.BlockSpec(memory_space=pl.ANY) for _ in loaded],
        ],
        out_specs=pl.BlockSpec((each, lags), lambda i: (0, 0)),
        out_shape=jax.ShapeDtypeStruct((each, lags), f32),
        scratch_shapes=[
            *[pltpu.VMEM(value.shape, value.dtype) for value in loaded],
            pltpu.VMEM((depth, LANES), jnp.int32),
            pltpu.VMEM((2 * channels, (blocks + COARSE) * LANES), bf16),
            pltpu.VMEM((REACH // LANES // COARSE * masks.shape[0], (blocks + COARSE) * LANES), f32),
            pltpu.VMEM((2, pairs, window * each, LANES), f32),
            pltpu.VMEM((pairs, window * each, LANES), f32),
            pltpu.VMEM((pairs, wide, LANES), f32),
            pltpu.VMEM((pairs, wide, LANES), f32),
            pltpu.VMEM((outer * each, LANES), f32),
            pltpu.VMEM((lags // LANES * each, LANES), f32),
            pltpu.SemaphoreType.DMA((len(loaded),)),
            *[pltpu.SemaphoreType.DMA((pairs,)) for _ in range(4)],
        ],
        compiler_params=pltpu.CompilerParams(collective_id=0, has_side_effects=True),
        name="detect",
    )(moveouts[None, :], moveouts[None, :], traces, *loaded)


def solution(mesh):
    return jax.shard_map(
        functools.partial(on_device, mesh.shape["tm"]),
        mesh=mesh,
        in_specs=(P("grp", "tm"), P("tm", None), P("grp"), P(None, "grp")),
        out_specs=P("tm", "grp"),
        check_vma=False,
    )
```

profile of v0, /device:TPU:11, one launch (start us, length us, event | category | flops | bytes accessed | tf_op | source)
XLA Modules:
  0.0 27.0 jit_solution(6212534600668766674)
XLA Ops:
  0.0 25.4 %detect.1 = f32[4,8192]{1,0:T(4,128)} custom-call(s32[1,1024]{1,0:T(1,128)} %bitcast.1, s32[1,1024]{1,0:T(1,128)} %bitcast.2, f32[1024,1024]{1,0:T(8,128)} %traces_ref.1, s32[64,1024]{1,0:T(8,128)} %mask_hbm.1, f32[4,8192]{1,0:T(4,128)} %template_hbm.1, bf16[256,384]{1,0:T(8,128)(2,1)} %constant.10.clone.first_hbm, ...), custom_call_target="tpu_custom_call" | custom-call | tf_op jit(solution)/shard_map/detect/pallas_call | solution.py:344
  25.4 1.6 %copy.11 = f32[4,8192]{1,0:T(4,128)} copy(f32[4,8192]{1,0:T(4,128)} %detect.1) | data formatting | bytes 262144
where the time goes:
time: 27.1 us; the launch traced here: 27 us
  Pallas kernels  25.4 us (94%)
  local copies, waits for them, and re-layouts  1.57 us (6%)
    pallas_call x1, Pallas kernels, on_device(): pl.pallas_call(functools.partial(kernel, devices, channels), grid=(channe...  25.4 us
    unnamed x1, local copies, waits for them, and re-layouts  1.57 us

commit v1 on v0

--- a/solution.py
+++ b/solution.py
@@ -104,23 +104,31 @@
     part,
     arrived,
     merged,
+    beside,
     joined,
     series,
     tail,
     load_sem,
     pair_send,
     pair_recv,
-    send_sem,
-    recv_sem,
+    beside_send,
+    beside_recv,
+    own_send,
+    own_recv,
+    sum_send,
+    sum_recv,
 ):
     step = pl.program_id(0)
     steps = pl.num_programs(0)
     depth, width = traces_ref.shape
     each, lags = template_ref.shape
     pairs = devices // 2
+    quads = devices // 4
     me = lax.axis_index("tm")
     core = lax.rem(me, 2)
     pair = me // 2
+    quad = pair // 2
+    side = lax.rem(pair, 2)
     partner = me + 1 - 2 * core
     blocks = width // LANES
     window = blocks + REACH // LANES
@@ -165,9 +173,6 @@
 
     lax.fori_loop(0, depth // 64, four_groups, 0)
 
-    def peer(k):
-        return lax.rem(pair + 1 + k, pairs)
-
     def to_partner(g):
         return pltpu.make_async_remote_copy(
             src_ref=part.at[1 - core, g],
@@ -178,16 +183,61 @@
             device_id_type=pl.DeviceIdType.MESH,
         )
 
-    def to_owner(k):
-        g = peer(k)
+    common, alone = REACH // LANES * each, 2 * blocks * each
+    common_at = pl.multiple_of((1 - side) * alone, each)
+    alone_at = pl.multiple_of(side * common, each)
+
+    def to_beside(q):
         return pltpu.make_async_remote_copy(
-            src_ref=merged.at[g],
-            dst_ref=joined.at[pair],
-            send_sem=send_sem.at[k],
-            recv_sem=recv_sem.at[k],
+            src_ref=merged.at[2 * q + 1 - side, pl.ds(common_at, common)],
+            dst_ref=beside.at[q],
+            send_sem=beside_send.at[q],
+            recv_sem=beside_recv.at[q],
+            device_id={"tm": 2 * (2 * quad + 1 - side) + core},
+            device_id_type=pl.DeviceIdType.MESH,
+        )
+
+    def alone_copy(g, source_quad, source_side):
+        return pltpu.make_async_remote_copy(
+            src_ref=merged.at[g, pl.ds(alone_at, alone)],
+            dst_ref=joined.at[
+                source_quad, pl.ds(pl.multiple_of(source_side * (alone + common), each), alone)
+            ],
+            send_sem=own_send.at[g],
+            recv_sem=own_recv.at[2 * source_quad + source_side],
             device_id={"tm": 2 * g + core},
             device_id_type=pl.DeviceIdType.MESH,
         )
+
+    def sum_copy(q, source_quad):
+        return pltpu.make_async_remote_copy(
+            src_ref=merged.at[2 * q + side, pl.ds(common_at, common)],
+            dst_ref=joined.at[source_quad, alone : alone + common],
+            send_sem=sum_send.at[q],
+            recv_sem=sum_recv.at[source_quad],
+            device_id={"tm": 2 * (2 * q + side) + core},
+            device_id_type=pl.DeviceIdType.MESH,
+        )
+
+    half = quads // 2
+
+    def far(k):
+        return (1 - quad // half) * half + lax.rem(quad + k, half)
+
+    def near(k):
+        return quad // half * half + lax.rem(quad + k, half)
+
+    def in_order(body):
+        def across(k, _):
+            body(far(k))
+            return 0
+
+        def around(k, _):
+            body(near(k))
+            return 0
+
+        lax.fori_loop(0, half, across, 0)
+        lax.fori_loop(1, half, around, 0)
 
     @pl.when(step == steps - 1)
     def _():
@@ -222,12 +272,12 @@
                 )
         pl.semaphore_wait(barrier, pairs)
 
-        def first_send(k, _):
-            to_partner(peer(k)).start()
-            return 0
-
-        lax.fori_loop(0, pairs - 1, first_send, 0)
-        to_partner(pair).start()
+        def first_send(q):
+            to_partner(2 * q + 1 - side).start()
+            to_partner(2 * q + side).start()
+
+        in_order(first_send)
+        first_send(quad)
         rows, more = window * each, blocks * each
 
         def merge(g):
@@ -235,23 +285,22 @@
             own, other = part[core, g], arrived[g]
             early = jnp.where(core == 0, own, other)
             later = jnp.where(core == 0, other, own)
-            middle = early[more:] + later[: rows - more]
-            return early[:more], middle, later[rows - more :]
-
-        def second_send(k, _):
-            g = peer(k)
-            begin, middle, end = merge(g)
-            merged[g, 0:more] = begin
-            merged[g, more:rows] = middle
-            merged[g, rows : rows + more] = end
-            to_owner(k).start()
-            return 0
-
-        lax.fori_loop(0, pairs - 1, second_send, 0)
-        begin, middle, end = merge(pair)
-        joined[pair, 0:more] = begin
-        joined[pair, more:rows] = middle
-        joined[pair, rows : rows + more] = end
+            merged[g, 0:more] = early[:more]
+            merged[g, more:rows] = early[more:] + later[: rows - more]
+            merged[g, rows : rows + more] = later[rows - more :]
+
+        def second_send(q):
+            merge(2 * q + 1 - side)
+            to_beside(q).start()
+            alone_copy(2 * q + 1 - side, quad, side).start()
+            merge(2 * q + side)
+            alone_copy(2 * q + side, quad, side).start()
+
+        in_order(second_send)
+        merge(2 * quad + 1 - side)
+        to_beside(quad).start()
+        alone_copy(2 * quad + 1 - side, quad, side).start()
+        merge(pair)
 
         for load in loads[1:]:
             load.wait()
@@ -269,11 +318,31 @@
 
         templ = transform(columns(), first_ref, forward_ref, cosine, sine)
 
-        def finish(k, _):
-            to_owner(k).wait()
-            return 0
-
-        lax.fori_loop(0, pairs - 1, finish, 0)
+        def add_beside(q):
+            to_beside(q).wait_recv()
+            here = (2 * q + side, pl.ds(common_at, common))
+            merged[here] = merged[here] + beside[q]
+
+        def third_send(q):
+            add_beside(q)
+            sum_copy(q, quad).start()
+
+        in_order(third_send)
+        add_beside(quad)
+        joined[quad, alone : alone + common] = merged[pair, pl.ds(common_at, common)]
+        joined[quad, pl.ds(pl.multiple_of(side * (alone + common), each), alone)] = merged[
+            pair, pl.ds(alone_at, alone)
+        ]
+
+        def finish(q):
+            alone_copy(2 * q + 1 - side, q, 1 - side).wait()
+            alone_copy(2 * q + side, q, side).wait()
+            to_beside(q).wait_send()
+            sum_copy(q, q).wait()
+
+        in_order(finish)
+        alone_copy(2 * quad + 1 - side, quad, 1 - side).wait()
+        to_beside(quad).wait_send()
 
         def leave(g, _):
             to_partner(g).wait_send()
@@ -282,11 +351,11 @@
         lax.fori_loop(0, pairs, leave, 0)
         series[...] = jnp.zeros(series.shape, f32)
         local = 2 * blocks
-        wide = window + blocks
-        for source in range(pairs):
+        wide = 2 * local + REACH // LANES
+        for source in range(quads):
             for b in range(0, wide, local):
                 taken = min(local, wide - b)
-                block = (source * local + b - REACH // LANES) % outer
+                block = (2 * source * local + b - REACH // LANES) % outer
                 here = slice(block * each, (block + taken) * each)
                 series[here, :] = series[here, :] + joined[source, b * each : (b + taken) * each, :]
         stack = transform(columns(), first_ref, forward_ref, cosine, sine)
@@ -338,9 +407,9 @@
     outer = devices * blocks
     window = blocks + REACH // LANES
     depth = math.gcd(channels, 256)
-    pairs = devices // 2
+    pairs, quads = devices // 2, devices // 4
     loaded = [masks, templates, *[jnp.asarray(table) for table in tables(outer * LANES, lags)]]
-    wide = (window + blocks) * each
+    alone, common = 2 * blocks * each, REACH // LANES * each
     return pl.pallas_call(
         functools.partial(kernel, devices, channels),
         grid=(channels // depth,),
@@ -359,12 +428,13 @@
             pltpu.VMEM((REACH // LANES // COARSE * masks.shape[0], (blocks + COARSE) * LANES), f32),
             pltpu.VMEM((2, pairs, window * each, LANES), f32),
             pltpu.VMEM((pairs, window * each, LANES), f32),
-            pltpu.VMEM((pairs, wide, LANES), f32),
-            pltpu.VMEM((pairs, wide, LANES), f32),
+            pltpu.VMEM((pairs, alone + common, LANES), f32),
+            pltpu.VMEM((quads, common, LANES), f32),
+            pltpu.VMEM((quads, 2 * alone + common, LANES), f32),
             pltpu.VMEM((outer * each, LANES), f32),
             pltpu.VMEM((lags // LANES * each, LANES), f32),
             pltpu.SemaphoreType.DMA((len(loaded),)),
-            *[pltpu.SemaphoreType.DMA((pairs,)) for _ in range(4)],
+            *[pltpu.SemaphoreType.DMA((count,)) for count in (pairs, pairs, quads, quads, pairs, pairs, quads, quads)],
         ],
         compiler_params=pltpu.CompilerParams(collective_id=0, has_side_effects=True),
         name="detect",

time: 27.1 us -> 26.2 us (0.967)
  the two profiles are of different devices: /device:TPU:11 before, /device:TPU:0 now
where the time goes in v1:
time: 26.2 us; the launch traced here: 26 us
  Pallas kernels  24.5 us (94%)
  local copies, waits for them, and re-layouts  1.57 us (6%)
    pallas_call x1, Pallas kernels, on_device(): pl.pallas_call(functools.partial(kernel, devices, channels), grid=(channe...  24.5 us
    unnamed x1, local copies, waits for them, and re-layouts  1.57 us

profile of v1, /device:TPU:0, one launch (start us, length us, event | category | flops | bytes accessed | tf_op | source)
XLA Modules:
  0.0 26.0 jit_solution(9051225366893300319)
XLA Ops:
  0.0 24.5 %detect.1 = f32[4,8192]{1,0:T(4,128)} custom-call(s32[1,1024]{1,0:T(1,128)} %bitcast.1, s32[1,1024]{1,0:T(1,128)} %bitcast.2, f32[1024,1024]{1,0:T(8,128)} %traces_ref.1, s32[64,1024]{1,0:T(8,128)} %mask_hbm.1, f32[4,8192]{1,0:T(4,128)} %template_hbm.1, bf16[256,384]{1,0:T(8,128)(2,1)} %constant.10.clone.first_hbm, ...), custom_call_target="tpu_custom_call" | custom-call | tf_op jit(solution)/shard_map/detect/pallas_call | solution.py:413
  24.5 1.6 %copy.11 = f32[4,8192]{1,0:T(4,128)} copy(f32[4,8192]{1,0:T(4,128)} %detect.1) | data formatting | bytes 262144

commit v2 on v1

v2 whole, which is shorter than its diff:
```python
import functools
import math

import jax
import jax.numpy as jnp
import numpy as np
from jax import lax
from jax.experimental import pallas as pl
from jax.experimental.pallas import tpu as pltpu
from jax.sharding import PartitionSpec as P

f32, bf16 = jnp.float32, jnp.bfloat16
LANES = 128
REACH = 2048
COARSE = 4


def split(value):
    high = value.astype(bf16)
    return high, (value - high.astype(f32)).astype(bf16)


def split_table(table):
    high = table.astype(jnp.bfloat16)
    return high, (table - high.astype(np.float64)).astype(jnp.bfloat16)


def transform(rows, first_ref, forward_ref, cosine, sine):
    outer = cosine.shape[0]
    high, low = split(jnp.concatenate(rows, axis=1))
    first = jnp.dot(first_ref[...], jnp.concatenate([high, high, low], axis=0), preferred_element_type=f32)
    turned = []
    for r in range(len(rows)):
        re = first[:outer, r * LANES : (r + 1) * LANES]
        im = first[outer:, r * LANES : (r + 1) * LANES]
        turned.append(jnp.concatenate([re * cosine + im * sine, im * cosine - re * sine], axis=1))
    high, low = split(jnp.concatenate(turned, axis=0))
    return jnp.dot(jnp.concatenate([high, low, high], axis=1), forward_ref[...], preferred_element_type=f32)


def shift(traces, late, terms, row, target, depth):
    rows = 16
    blocks = traces.shape[1] // LANES
    here = slice(row, row + rows)
    delay = late[here, :]
    lane = lax.broadcasted_iota(jnp.int32, (rows, LANES), 1)
    inner = (delay & (LANES - 1)) + 1
    index = (lane - inner) & (LANES - 1)
    keep = lane >= inner
    turned = [
        jnp.take_along_axis(traces[here, b * LANES : (b + 1) * LANES], index, axis=1, mode="promise_in_bounds")
        for b in range(blocks)
    ]
    zero = jnp.zeros((rows, LANES), f32)
    moved = [
        jnp.where(keep, turned[b] if b < blocks else zero, turned[b - 1] if b > 0 else zero)
        for b in range(blocks + 1)
    ]
    hop = 1
    while hop < COARSE:
        chosen = ((delay // LANES) & hop) != 0
        moved = [
            jnp.where(
                chosen,
                moved[b - hop] if b >= hop else zero,
                moved[b] if b < len(moved) else zero,
            )
            for b in range(len(moved) + hop)
        ]
        hop *= 2
    for b in range(len(moved)):
        high, low = split(moved[b])
        column = slice(b * LANES, (b + 1) * LANES)
        terms[target : target + rows, column] = high
        terms[target + depth : target + depth + rows, column] = low


def kernel(
    devices,
    channels,
    moveouts_hbm,
    mask_hbm,
    traces_hbm,
    template_hbm,
    first_hbm,
    forward_hbm,
    back_hbm,
    last_hbm,
    twiddle_hbm,
    out_ref,
    moveouts_ref,
    mask_ref,
    template_ref,
    first_ref,
    forward_ref,
    back_ref,
    last_ref,
    twiddle_ref,
    traces,
    late,
    chosen,
    terms,
    raw,
    part,
    arrived,
    merged,
    beside,
    joined,
    series,
    tail,
    load_sem,
    trace_sem,
    pair_send,
    pair_recv,
    beside_send,
    beside_recv,
    own_send,
    own_recv,
    sum_send,
    sum_recv,
):
    width = traces.shape[1]
    depth = math.gcd(channels, 256)
    each, lags = template_ref.shape
    pairs = devices // 2
    quads = devices // 4
    me = lax.axis_index("tm")
    core = lax.rem(me, 2)
    pair = me // 2
    quad = pair // 2
    side = lax.rem(pair, 2)
    partner = me + 1 - 2 * core
    blocks = width // LANES
    window = blocks + REACH // LANES
    outer = devices * blocks
    loads = [
        pltpu.make_async_copy(source, target, load_sem.at[i])
        for i, (source, target) in enumerate(
            (
                (moveouts_hbm, moveouts_ref),
                (mask_hbm, mask_ref),
                (template_hbm, template_ref),
                (first_hbm, first_ref),
                (forward_hbm, forward_ref),
                (twiddle_hbm, twiddle_ref),
                (back_hbm, back_ref),
                (last_hbm, last_ref),
            )
        )
    ]
    barrier = pltpu.get_barrier_semaphore()

    fetches = [
        pltpu.make_async_copy(
            traces_hbm.at[p * LANES : (p + 1) * LANES], traces.at[p * LANES : (p + 1) * LANES], trace_sem.at[p]
        )
        for p in range(channels // LANES)
    ]
    for load in loads[:2] + fetches + loads[2:]:
        load.start()

    def greet(i, _):
        target = 2 * lax.rem(pair + i, pairs) + core
        pl.semaphore_signal(barrier, inc=1, device_id={"tm": target}, device_id_type=pl.DeviceIdType.MESH)
        return 0

    pl.semaphore_signal(barrier, inc=1, device_id={"tm": partner}, device_id_type=pl.DeviceIdType.MESH)
    lax.fori_loop(1, pairs, greet, 0)

    def to_partner(g):
        return pltpu.make_async_remote_copy(
            src_ref=part.at[1 - core, g],
            dst_ref=arrived.at[g],
            send_sem=pair_send.at[g],
            recv_sem=pair_recv.at[g],
            device_id={"tm": partner},
            device_id_type=pl.DeviceIdType.MESH,
        )

    common, alone = REACH // LANES * each, 2 * blocks * each
    common_at = pl.multiple_of((1 - side) * alone, each)
    alone_at = pl.multiple_of(side * common, each)

    def to_beside(q):
        return pltpu.make_async_remote_copy(
            src_ref=merged.at[2 * q + 1 - side, pl.ds(common_at, common)],
            dst_ref=beside.at[q],
            send_sem=beside_send.at[q],
            recv_sem=beside_recv.at[q],
            device_id={"tm": 2 * (2 * quad + 1 - side) + core},
            device_id_type=pl.DeviceIdType.MESH,
        )

    def alone_copy(g, source_quad, source_side):
        return pltpu.make_async_remote_copy(
            src_ref=merged.at[g, pl.ds(alone_at, alone)],
            dst_ref=joined.at[
                source_quad, pl.ds(pl.multiple_of(source_side * (alone + common), each), alone)
            ],
            send_sem=own_send.at[g],
            recv_sem=own_recv.at[2 * source_quad + source_side],
            device_id={"tm": 2 * g + core},
            device_id_type=pl.DeviceIdType.MESH,
        )

    def sum_copy(q, source_quad):
        return pltpu.make_async_remote_copy(
            src_ref=merged.at[2 * q + side, pl.ds(common_at, common)],
            dst_ref=joined.at[source_quad, alone : alone + common],
            send_sem=sum_send.at[q],
            recv_sem=sum_recv.at[source_quad],
            device_id={"tm": 2 * (2 * q + side) + core},
            device_id_type=pl.DeviceIdType.MESH,
        )

    def in_order(body):
        def visit(q, _):
            body(q)
            return 0

        lax.fori_loop(0, quad, visit, 0)
        lax.fori_loop(quad + 1, quads, visit, 0)

    loads[0].wait()
    for p in range(channels // LANES):
        row = (REACH - 1) - moveouts_ref[:, p * LANES : (p + 1) * LANES]
        late[p * LANES : (p + 1) * LANES, :] = jnp.broadcast_to(row, (LANES, LANES)).T
    loads[1].wait()
    count = mask_ref.shape[0]
    coarse = ((REACH - 1) - moveouts_ref[...]) // (COARSE * LANES)
    hops = REACH // LANES // COARSE
    for h in range(hops):
        chosen[h * count : (h + 1) * count, :] = (
            jnp.where(coarse == h, mask_ref[...], 0).astype(f32).astype(bf16)
        )
    fine = blocks + COARSE
    span = 2 if fine % 2 == 0 else 1

    def combine(c):
        one = chosen[:, c * depth : (c + 1) * depth]
        double = jnp.concatenate([one, one], axis=1)
        for b in range(0, fine, span):
            column = slice(b * LANES, (b + span) * LANES)
            value = jnp.dot(
                double, terms[2 * c * depth : 2 * (c + 1) * depth, column], preferred_element_type=f32
            )
            raw[:, column] = value if c == 0 else raw[:, column] + value

    for c in range(channels // depth):
        for p in range(c * depth // LANES, (c + 1) * depth // LANES):
            fetches[p].wait()
        for row in range(0, depth, 16):
            shift(traces, late, terms, c * depth + row, 2 * c * depth + row, depth)
        if c > 0:
            combine(c - 1)
    combine(channels // depth - 1)

    def stacked(b):
        found = [h for h in range(hops) if 0 <= b - COARSE * h < fine]
        return sum(
            raw[h * count : (h + 1) * count, (b - COARSE * h) * LANES : (b - COARSE * h + 1) * LANES]
            for h in found
        )

    span = 2 if window % 2 == 0 else 1
    for b in range(0, window, span):
        added = [stacked(b + j) for j in range(span)]
        for owner in range(devices):
            part[owner % 2, owner // 2, b * each : (b + span) * each, :] = jnp.concatenate(
                [value[owner * each : (owner + 1) * each] for value in added], axis=0
            )
    pl.semaphore_wait(barrier, pairs)

    def first_send(q):
        to_partner(2 * q + 1 - side).start()
        to_partner(2 * q + side).start()

    in_order(first_send)
    first_send(quad)
    rows, more = window * each, blocks * each

    def merge(g):
        to_partner(g).wait_recv()
        own, other = part[core, g], arrived[g]
        early = jnp.where(core == 0, own, other)
        later = jnp.where(core == 0, other, own)
        merged[g, 0:more] = early[:more]
        merged[g, more:rows] = early[more:] + later[: rows - more]
        merged[g, rows : rows + more] = later[rows - more :]

    def second_send(q):
        merge(2 * q + 1 - side)
        to_beside(q).start()
        alone_copy(2 * q + 1 - side, quad, side).start()
        merge(2 * q + side)
        alone_copy(2 * q + side, quad, side).start()

    in_order(second_send)
    merge(2 * quad + 1 - side)
    to_beside(quad).start()
    alone_copy(2 * quad + 1 - side, quad, side).start()
    merge(pair)

    for load in loads[2:]:
        load.wait()
    cosine, sine = twiddle_ref[0], twiddle_ref[1]
    values = template_ref[...]
    count = lags // LANES
    for b in range(count):
        series[b * each : (b + 1) * each, :] = values[:, b * LANES : (b + 1) * LANES]
    series[count * each :, :] = jnp.zeros(((outer - count) * each, LANES), f32)
    energy = jnp.sqrt(jnp.sum(values * values, axis=1, keepdims=True) + 1e-06)
    factor = 1.0 / (outer * LANES * math.sqrt(channels) * energy)

    def columns():
        return [series[pl.ds(k, outer, stride=each), :] for k in range(each)]

    templ = transform(columns(), first_ref, forward_ref, cosine, sine)

    def add_beside(q):
        to_beside(q).wait_recv()
        here = (2 * q + side, pl.ds(common_at, common))
        merged[here] = merged[here] + beside[q]

    def third_send(q):
        add_beside(q)
        sum_copy(q, quad).start()

    in_order(third_send)
    add_beside(quad)
    joined[quad, alone : alone + common] = merged[pair, pl.ds(common_at, common)]
    joined[quad, pl.ds(pl.multiple_of(side * (alone + common), each), alone)] = merged[
        pair, pl.ds(alone_at, alone)
    ]

    def finish(q):
        alone_copy(2 * q + 1 - side, q, 1 - side).wait()
        alone_copy(2 * q + side, q, side).wait()
        to_beside(q).wait_send()
        sum_copy(q, q).wait()

    in_order(finish)
    alone_copy(2 * quad + 1 - side, quad, 1 - side).wait()
    to_beside(quad).wait_send()

    def leave(g, _):
        to_partner(g).wait_send()
        return 0

    lax.fori_loop(0, pairs, leave, 0)
    series[...] = jnp.zeros(series.shape, f32)
    local = 2 * blocks
    wide = 2 * local + REACH // LANES
    for source in range(quads):
        for b in range(0, wide, local):
            taken = min(local, wide - b)
            block = (2 * source * local + b - REACH // LANES) % outer
            here = slice(block * each, (block + taken) * each)
            series[here, :] = series[here, :] + joined[source, b * each : (b + taken) * each, :]
    stack = transform(columns(), first_ref, forward_ref, cosine, sine)
    stack_re, stack_im = stack[:, :LANES], stack[:, LANES:]
    templ_re, templ_im = templ[:, :LANES], templ[:, LANES:]
    product = jnp.concatenate(
        [stack_re * templ_re + stack_im * templ_im, stack_im * templ_re - stack_re * templ_im], axis=1
    )
    high, low = split(product)
    back = jnp.dot(jnp.concatenate([high, low, high], axis=1), back_ref[...], preferred_element_type=f32)
    turned = []
    for k in range(each):
        re = back[k * outer : (k + 1) * outer, :LANES]
        im = back[k * outer : (k + 1) * outer, LANES:]
        turned.append(jnp.concatenate([re * cosine - im * sine, re * sine + im * cosine], axis=0))
    high, low = split(jnp.concatenate(turned, axis=1))
    final = jnp.dot(last_ref[...], jnp.concatenate([high, high, low], axis=0), preferred_element_type=f32)
    for k in range(each):
        tail[pl.ds(k, count, stride=each), :] = final[:, k * LANES : (k + 1) * LANES]
    for b in range(count):
        out_ref[:, b * LANES : (b + 1) * LANES] = tail[b * each : (b + 1) * each, :] * factor


def tables(length, lags):
    outer = length // LANES
    turn = 2.0 * math.pi
    ramp = np.arange(outer)[:, None] * np.arange(outer)[None, :] % outer * (turn / outer)
    wide = np.arange(LANES)[:, None] * np.arange(LANES)[None, :] % LANES * (turn / LANES)
    twist = np.arange(outer)[:, None] * np.arange(LANES)[None, :] % length * (turn / length)
    first = split_table(np.concatenate([np.cos(ramp), -np.sin(ramp)], axis=0))
    cosine, sine = np.cos(wide), np.sin(wide)
    forward = split_table(np.block([[cosine, -sine], [sine, cosine]]))
    back = split_table(np.block([[cosine, sine], [-sine, cosine]]))
    shown = ramp[: lags // LANES]
    last = split_table(np.concatenate([np.cos(shown), -np.sin(shown)], axis=1))
    return (
        np.concatenate([first[0], first[1], first[0]], axis=1),
        np.concatenate([forward[0], forward[0], forward[1]], axis=0),
        np.concatenate([back[0], back[0], back[1]], axis=0),
        np.concatenate([last[0], last[1], last[0]], axis=1),
        np.stack([np.cos(twist), np.sin(twist)]).astype(np.float32),
    )


def on_device(devices, traces, templates, moveouts, masks):
    channels, width = traces.shape
    each, lags = templates.shape
    blocks = width // LANES
    outer = devices * blocks
    window = blocks + REACH // LANES
    pairs, quads = devices // 2, devices // 4
    loaded = [moveouts[None, :], masks, templates, *[jnp.asarray(table) for table in tables(outer * LANES, lags)]]
    alone, common = 2 * blocks * each, REACH // LANES * each
    return pl.pallas_call(
        functools.partial(kernel, devices, channels),
        in_specs=[pl.BlockSpec(memory_space=pl.ANY) for _ in range(len(loaded) + 1)],
        out_specs=pl.BlockSpec(memory_space=pltpu.VMEM),
        out_shape=pltpu.VMEM((each, lags), f32),
        scratch_shapes=[
            *[pltpu.VMEM(value.shape, value.dtype) for value in loaded],
            pltpu.VMEM((channels, width), f32),
            pltpu.VMEM((channels, LANES), jnp.int32),
            pltpu.VMEM((REACH // LANES // COARSE * masks.shape[0], channels), bf16),
            pltpu.VMEM((2 * channels, (blocks + COARSE) * LANES), bf16),
            pltpu.VMEM((REACH // LANES // COARSE * masks.shape[0], (blocks + COARSE) * LANES), f32),
            pltpu.VMEM((2, pairs, window * each, LANES), f32),
            pltpu.VMEM((pairs, window * each, LANES), f32),
            pltpu.VMEM((pairs, alone + common, LANES), f32),
            pltpu.VMEM((quads, common, LANES), f32),
            pltpu.VMEM((quads, 2 * alone + common, LANES), f32),
            pltpu.VMEM((outer * each, LANES), f32),
            pltpu.VMEM((lags // LANES * each, LANES), f32),
            pltpu.SemaphoreType.DMA((len(loaded),)),
            pltpu.SemaphoreType.DMA((channels // LANES,)),
            *[pltpu.SemaphoreType.DMA((count,)) for count in (pairs, pairs, quads, quads, pairs, pairs, quads, quads)],
        ],
        compiler_params=pltpu.CompilerParams(collective_id=0, has_side_effects=True),
        name="detect",
    )(*loaded[:2], traces, *loaded[2:])


def solution(mesh):
    return jax.shard_map(
        functools.partial(on_device, mesh.shape["tm"]),
        mesh=mesh,
        in_specs=(P("grp", "tm"), P("tm", None), P("grp"), P(None, "grp")),
        out_specs=P("tm", "grp"),
        check_vma=False,
    )
```

time: 26.2 us -> 21.4 us (0.82)
  Pallas kernels: 24.5 us -> 20.6 us
  local copies, waits for them, and re-layouts: 1.57 us -> 0.66 us
    pallas_call x1, Pallas kernels: 24.5 us -> 20.6 us  [on_device(): pl.pallas_call(functools.partial(kernel, devices, channels), in_specs=[pl...]
    unnamed x1, local copies, waits for them, and re-layouts: 1.57 us -> 0.66 us
where the time goes in v2:
time: 21.4 us; the launch traced here: 21.2 us
  Pallas kernels  20.6 us (96%)
  local copies, waits for them, and re-layouts  0.66 us (3%)
    pallas_call x1, Pallas kernels, on_device(): pl.pallas_call(functools.partial(kernel, devices, channels), in_specs=[pl...  20.6 us
    unnamed x1, local copies, waits for them, and re-layouts  0.66 us

profile of v2, /device:TPU:0, one launch (start us, length us, event | category | flops | bytes accessed | tf_op | source)
XLA Modules:
  0.0 21.2 jit_solution(4659201077334048724)
XLA Ops:
  0.0 20.6 %detect.1 = f32[4,8192]{1,0:T(4,128)S(1)} custom-call(s32[1,1024]{1,0:T(1,128)} %bitcast.1, s32[64,1024]{1,0:T(8,128)} %mask_hbm.1, f32[1024,1024]{1,0:T(8,128)} %traces_hbm.1, f32[4,8192]{1,0:T(4,128)} %template_hbm.1, bf16[256,384]{1,0:T(8,128)(2,1)} %constant.10.clone.first_hbm, bf16[768,256]{1,0:T(8,128)(2,1)} %constant.11.clone.forward_hbm, ...), custom_call_target="tpu_custom_call" | custom-call | tf_op jit(solution)/shard_map/detect/pallas_call | solution.py:411
  20.6 0.7 %copy.11 = f32[4,8192]{1,0:T(4,128)} copy(f32[4,8192]{1,0:T(4,128)S(1)} %detect.1) | data formatting | bytes 262144

commit v3 on v2

--- a/solution.py
+++ b/solution.py
@@ -39,7 +39,7 @@
 
 
 def shift(traces, late, terms, row, target, depth):
-    rows = 16
+    rows = 8
     blocks = traces.shape[1] // LANES
     here = slice(row, row + rows)
     delay = late[here, :]
@@ -68,9 +68,10 @@
             for b in range(len(moved) + hop)
         ]
         hop *= 2
-    for b in range(len(moved)):
-        high, low = split(moved[b])
-        column = slice(b * LANES, (b + 1) * LANES)
+    span = 2 if len(moved) % 2 == 0 else 1
+    for b in range(0, len(moved), span):
+        high, low = split(jnp.concatenate(moved[b : b + span], axis=1))
+        column = slice(b * LANES, (b + span) * LANES)
         terms[target : target + rows, column] = high
         terms[target + depth : target + depth + rows, column] = low
 
@@ -156,7 +157,8 @@
         )
         for p in range(channels // LANES)
     ]
-    for load in loads[:2] + fetches + loads[2:]:
+    first_rows = depth // LANES
+    for load in loads[:1] + fetches[:first_rows] + loads[1:2] + fetches[first_rows:] + loads[2:]:
         load.start()
 
     def greet(i, _):
@@ -225,14 +227,17 @@
     for p in range(channels // LANES):
         row = (REACH - 1) - moveouts_ref[:, p * LANES : (p + 1) * LANES]
         late[p * LANES : (p + 1) * LANES, :] = jnp.broadcast_to(row, (LANES, LANES)).T
-    loads[1].wait()
     count = mask_ref.shape[0]
-    coarse = ((REACH - 1) - moveouts_ref[...]) // (COARSE * LANES)
     hops = REACH // LANES // COARSE
-    for h in range(hops):
-        chosen[h * count : (h + 1) * count, :] = (
-            jnp.where(coarse == h, mask_ref[...], 0).astype(f32).astype(bf16)
-        )
+
+    def choose():
+        loads[1].wait()
+        coarse = ((REACH - 1) - moveouts_ref[...]) // (COARSE * LANES)
+        for h in range(hops):
+            chosen[h * count : (h + 1) * count, :] = (
+                jnp.where(coarse == h, mask_ref[...], 0).astype(f32).astype(bf16)
+            )
+
     fine = blocks + COARSE
     span = 2 if fine % 2 == 0 else 1
 
@@ -249,10 +254,14 @@
     for c in range(channels // depth):
         for p in range(c * depth // LANES, (c + 1) * depth // LANES):
             fetches[p].wait()
-        for row in range(0, depth, 16):
+        if c == 1:
+            choose()
+        for row in range(0, depth, 8):
             shift(traces, late, terms, c * depth + row, 2 * c * depth + row, depth)
         if c > 0:
             combine(c - 1)
+    if channels == depth:
+        choose()
     combine(channels // depth - 1)
 
     def stacked(b):
@@ -288,12 +297,22 @@
         merged[g, more:rows] = early[more:] + later[: rows - more]
         merged[g, rows : rows + more] = later[rows - more :]
 
+    def alone_send(q):
+        alone_copy(2 * q + 1 - side, quad, side).start()
+        alone_copy(2 * q + side, quad, side).start()
+
     def second_send(q):
         merge(2 * q + 1 - side)
         to_beside(q).start()
-        alone_copy(2 * q + 1 - side, quad, side).start()
         merge(2 * q + side)
-        alone_copy(2 * q + side, quad, side).start()
+
+        @pl.when((q == 0) | (q > quad))
+        def _():
+            alone_copy(2 * q + side, quad, side).start()
+
+        @pl.when(q == 0)
+        def _():
+            alone_copy(2 * q + 1 - side, quad, side).start()
 
     in_order(second_send)
     merge(2 * quad + 1 - side)
@@ -326,7 +345,17 @@
         add_beside(q)
         sum_copy(q, quad).start()
 
+        @pl.when(q + 1 < quad)
+        def _():
+            alone_send(q + 1)
+
     in_order(third_send)
+
+    def fourth_send(q, _):
+        alone_copy(2 * q + 1 - side, quad, side).start()
+        return 0
+
+    lax.fori_loop(quad + 1, quads, fourth_send, 0)
     add_beside(quad)
     joined[quad, alone : alone + common] = merged[pair, pl.ds(common_at, common)]
     joined[quad, pl.ds(pl.multiple_of(side * (alone + common), each), alone)] = merged[

time: 21.4 us -> 20.2 us (0.944)
  Pallas kernels: 20.6 us -> 19.4 us
    pallas_call x1, Pallas kernels: 20.6 us -> 19.4 us  [on_device(): pl.pallas_call(functools.partial(kernel, devices, channels), in_specs=[pl...]
where the time goes in v3:
time: 20.2 us; the launch traced here: 20.1 us
  Pallas kernels  19.4 us (96%)
  local copies, waits for them, and re-layouts  0.66 us (3%)
    pallas_call x1, Pallas kernels, on_device(): pl.pallas_call(functools.partial(kernel, devices, channels), in_specs=[pl...  19.4 us
    unnamed x1, local copies, waits for them, and re-layouts  0.66 us

profile of v3, /device:TPU:0, one launch (start us, length us, event | category | flops | bytes accessed | tf_op | source)
XLA Modules:
  0.0 20.1 jit_solution(5467727639029658715)
XLA Ops:
  0.0 19.4 %detect.1 = f32[4,8192]{1,0:T(4,128)S(1)} custom-call(s32[1,1024]{1,0:T(1,128)} %bitcast.1, s32[64,1024]{1,0:T(8,128)} %mask_hbm.1, f32[1024,1024]{1,0:T(8,128)} %traces_hbm.1, f32[4,8192]{1,0:T(4,128)} %template_hbm.1, bf16[256,384]{1,0:T(8,128)(2,1)} %constant.10.clone.first_hbm, bf16[768,256]{1,0:T(8,128)(2,1)} %constant.11.clone.forward_hbm, ...), custom_call_target="tpu_custom_call" | custom-call | tf_op jit(solution)/shard_map/detect/pallas_call | solution.py:440
  19.4 0.7 %copy.11 = f32[4,8192]{1,0:T(4,128)} copy(f32[4,8192]{1,0:T(4,128)S(1)} %detect.1) | data formatting | bytes 262144

commit v4 on v3

--- a/solution.py
+++ b/solution.py
@@ -297,16 +297,14 @@
         merged[g, more:rows] = early[more:] + later[: rows - more]
         merged[g, rows : rows + more] = later[rows - more :]
 
-    def alone_send(q):
-        alone_copy(2 * q + 1 - side, quad, side).start()
-        alone_copy(2 * q + side, quad, side).start()
+    early = jnp.where(quad == quads // 2, quad, 0)
 
     def second_send(q):
         merge(2 * q + 1 - side)
         to_beside(q).start()
         merge(2 * q + side)
 
-        @pl.when((q == 0) | (q > quad))
+        @pl.when((q == 0) | (q > quad) | (q + 1 == early))
         def _():
             alone_copy(2 * q + side, quad, side).start()
 
@@ -323,6 +321,7 @@
     for load in loads[2:]:
         load.wait()
     cosine, sine = twiddle_ref[0], twiddle_ref[1]
+    kept = cosine.shape[0]
     values = template_ref[...]
     count = lags // LANES
     for b in range(count):
@@ -345,17 +344,21 @@
         add_beside(q)
         sum_copy(q, quad).start()
 
+        @pl.when((q + 1 < quad) & (q + 2 != early))
+        def _():
+            alone_copy(2 * (q + 1) + side, quad, side).start()
+
         @pl.when(q + 1 < quad)
         def _():
-            alone_send(q + 1)
-
-    in_order(third_send)
+            alone_copy(2 * (q + 1) + 1 - side, quad, side).start()
 
     def fourth_send(q, _):
         alone_copy(2 * q + 1 - side, quad, side).start()
         return 0
 
     lax.fori_loop(quad + 1, quads, fourth_send, 0)
+    in_order(third_send)
+
     add_beside(quad)
     joined[quad, alone : alone + common] = merged[pair, pl.ds(common_at, common)]
     joined[quad, pl.ds(pl.multiple_of(side * (alone + common), each), alone)] = merged[
@@ -396,8 +399,8 @@
     back = jnp.dot(jnp.concatenate([high, low, high], axis=1), back_ref[...], preferred_element_type=f32)
     turned = []
     for k in range(each):
-        re = back[k * outer : (k + 1) * outer, :LANES]
-        im = back[k * outer : (k + 1) * outer, LANES:]
+        re = back[k * kept : (k + 1) * kept, :LANES]
+        im = back[k * kept : (k + 1) * kept, LANES:]
         turned.append(jnp.concatenate([re * cosine - im * sine, re * sine + im * cosine], axis=0))
     high, low = split(jnp.concatenate(turned, axis=1))
     final = jnp.dot(last_ref[...], jnp.concatenate([high, high, low], axis=0), preferred_element_type=f32)
@@ -410,15 +413,17 @@
 def tables(length, lags):
     outer = length // LANES
     turn = 2.0 * math.pi
-    ramp = np.arange(outer)[:, None] * np.arange(outer)[None, :] % outer * (turn / outer)
+    kept = (outer // 2 + 1 + 7) // 8 * 8
+    weight = np.where(np.arange(kept) % (outer // 2) == 0, 1.0, 2.0) * (np.arange(kept) <= outer // 2)
+    ramp = np.arange(kept)[:, None] * np.arange(outer)[None, :] % outer * (turn / outer)
     wide = np.arange(LANES)[:, None] * np.arange(LANES)[None, :] % LANES * (turn / LANES)
-    twist = np.arange(outer)[:, None] * np.arange(LANES)[None, :] % length * (turn / length)
+    twist = np.arange(kept)[:, None] * np.arange(LANES)[None, :] % length * (turn / length)
     first = split_table(np.concatenate([np.cos(ramp), -np.sin(ramp)], axis=0))
     cosine, sine = np.cos(wide), np.sin(wide)
     forward = split_table(np.block([[cosine, -sine], [sine, cosine]]))
     back = split_table(np.block([[cosine, sine], [-sine, cosine]]))
-    shown = ramp[: lags // LANES]
-    last = split_table(np.concatenate([np.cos(shown), -np.sin(shown)], axis=1))
+    shown = ramp[:, : lags // LANES].T
+    last = split_table(np.concatenate([np.cos(shown) * weight, -np.sin(shown) * weight], axis=1))
     return (
         np.concatenate([first[0], first[1], first[0]], axis=1),
         np.concatenate([forward[0], forward[0], forward[1]], axis=0),

time: 20.2 us -> 19.8 us (0.980)
  Pallas kernels: 19.4 us -> 19 us
    pallas_call x1, Pallas kernels: 19.4 us -> 19 us  [on_device(): pl.pallas_call(functools.partial(kernel, devices, channels), in_specs=[pl...]
where the time goes in v4:
time: 19.8 us; the launch traced here: 19.6 us
  Pallas kernels  19 us (96%)
  local copies, waits for them, and re-layouts  0.66 us (3%)
    pallas_call x1, Pallas kernels, on_device(): pl.pallas_call(functools.partial(kernel, devices, channels), in_specs=[pl...  19 us
    unnamed x1, local copies, waits for them, and re-layouts  0.66 us

profile of v4, /device:TPU:0, one launch (start us, length us, event | category | flops | bytes accessed | tf_op | source)
XLA Modules:
  0.0 19.6 jit_solution(17171268493791560310)
XLA Ops:
  0.0 19.0 %detect.1 = f32[4,8192]{1,0:T(4,128)S(1)} custom-call(s32[1,1024]{1,0:T(1,128)} %bitcast.1, s32[64,1024]{1,0:T(8,128)} %mask_hbm.1, f32[1024,1024]{1,0:T(8,128)} %traces_hbm.1, f32[4,8192]{1,0:T(4,128)} %template_hbm.1, bf16[144,384]{1,0:T(8,128)(2,1)} %constant.10.clone.first_hbm, bf16[768,256]{1,0:T(8,128)(2,1)} %constant.11.clone.forward_hbm, ...), custom_call_target="tpu_custom_call" | custom-call | tf_op jit(solution)/shard_map/detect/pallas_call | solution.py:445
  19.0 0.7 %copy.11 = f32[4,8192]{1,0:T(4,128)} copy(f32[4,8192]{1,0:T(4,128)S(1)} %detect.1) | data formatting | bytes 262144

commit v5 on v4

--- a/solution.py
+++ b/solution.py
@@ -297,20 +297,24 @@
         merged[g, more:rows] = early[more:] + later[: rows - more]
         merged[g, rows : rows + more] = later[rows - more :]
 
-    early = jnp.where(quad == quads // 2, quad, 0)
+    half = quads // 2
+
+    def at_once(q):
+        return (q < quad) & ((q == 0) | ((q < half) & (quad > half)))
 
     def second_send(q):
         merge(2 * q + 1 - side)
         to_beside(q).start()
         merge(2 * q + side)
 
-        @pl.when((q == 0) | (q > quad) | (q + 1 == early))
+        @pl.when(q > quad)
         def _():
             alone_copy(2 * q + side, quad, side).start()
 
-        @pl.when(q == 0)
+        @pl.when(at_once(q))
         def _():
-            alone_copy(2 * q + 1 - side, quad, side).start()
+            alone_copy(2 * q, quad, side).start()
+            alone_copy(2 * q + 1, quad, side).start()
 
     in_order(second_send)
     merge(2 * quad + 1 - side)
@@ -344,12 +348,9 @@
         add_beside(q)
         sum_copy(q, quad).start()
 
-        @pl.when((q + 1 < quad) & (q + 2 != early))
+        @pl.when((q + 1 < quad) & jnp.logical_not(at_once(q + 1)))
         def _():
             alone_copy(2 * (q + 1) + side, quad, side).start()
-
-        @pl.when(q + 1 < quad)
-        def _():
             alone_copy(2 * (q + 1) + 1 - side, quad, side).start()
 
     def fourth_send(q, _):
@@ -365,6 +366,13 @@
         pair, pl.ds(alone_at, alone)
     ]
 
+    def leave(g, _):
+        to_partner(g).wait_send()
+        return 0
+
+    lax.fori_loop(0, pairs, leave, 0)
+    series[...] = jnp.zeros(series.shape, f32)
+
     def finish(q):
         alone_copy(2 * q + 1 - side, q, 1 - side).wait()
         alone_copy(2 * q + side, q, side).wait()
@@ -375,12 +383,6 @@
     alone_copy(2 * quad + 1 - side, quad, 1 - side).wait()
     to_beside(quad).wait_send()
 
-    def leave(g, _):
-        to_partner(g).wait_send()
-        return 0
-
-    lax.fori_loop(0, pairs, leave, 0)
-    series[...] = jnp.zeros(series.shape, f32)
     local = 2 * blocks
     wide = 2 * local + REACH // LANES
     for source in range(quads):

time: 19.8 us -> 19.5 us (0.985); the launches traced: 19.6 us -> 19.1 us
  Pallas kernels: 19 us -> 18.4 us
    pallas_call x1, Pallas kernels: 19 us -> 18.4 us  [on_device(): pl.pallas_call(functools.partial(kernel, devices, channels), in_specs=[pl...]
where the time goes in v5:
time: 19.5 us; the launch traced here: 19.1 us
  Pallas kernels  18.4 us (94%)
  local copies, waits for them, and re-layouts  0.66 us (3%)
    pallas_call x1, Pallas kernels, on_device(): pl.pallas_call(functools.partial(kernel, devices, channels), in_specs=[pl...  18.4 us
    unnamed x1, local copies, waits for them, and re-layouts  0.66 us

profile of v5, /device:TPU:0, one launch (start us, length us, event | category | flops | bytes accessed | tf_op | source)
XLA Modules:
  0.0 19.1 jit_solution(2577023497131822545)
XLA Ops:
  0.0 18.4 %detect.1 = f32[4,8192]{1,0:T(4,128)S(1)} custom-call(s32[1,1024]{1,0:T(1,128)} %bitcast.1, s32[64,1024]{1,0:T(8,128)} %mask_hbm.1, f32[1024,1024]{1,0:T(8,128)} %traces_hbm.1, f32[4,8192]{1,0:T(4,128)} %template_hbm.1, bf16[144,384]{1,0:T(8,128)(2,1)} %constant.10.clone.first_hbm, bf16[768,256]{1,0:T(8,128)(2,1)} %constant.11.clone.forward_hbm, ...), custom_call_target="tpu_custom_call" | custom-call | tf_op jit(solution)/shard_map/detect/pallas_call | solution.py:447
  18.5 0.7 %copy.11 = f32[4,8192]{1,0:T(4,128)} copy(f32[4,8192]{1,0:T(4,128)S(1)} %detect.1) | data formatting | bytes 262144

commit v6 on v5

--- a/solution.py
+++ b/solution.py
@@ -350,8 +350,8 @@
 
         @pl.when((q + 1 < quad) & jnp.logical_not(at_once(q + 1)))
         def _():
+            alone_copy(2 * (q + 1) + 1 - side, quad, side).start()
             alone_copy(2 * (q + 1) + side, quad, side).start()
-            alone_copy(2 * (q + 1) + 1 - side, quad, side).start()
 
     def fourth_send(q, _):
         alone_copy(2 * q + 1 - side, quad, side).start()

time: 19.5 us -> 19.3 us (0.990); the launches traced: 19.1 us -> 19.1 us
  no operation moved by 1% of the time
where the time goes in v6:
time: 19.3 us; the launch traced here: 19.1 us
  Pallas kernels  18.4 us (95%)
  local copies, waits for them, and re-layouts  0.66 us (3%)
    pallas_call x1, Pallas kernels, on_device(): pl.pallas_call(functools.partial(kernel, devices, channels), in_specs=[pl...  18.4 us
    unnamed x1, local copies, waits for them, and re-layouts  0.66 us

profile of v6, /device:TPU:0, one launch (start us, length us, event | category | flops | bytes accessed | tf_op | source)
XLA Modules:
  0.0 19.1 jit_solution(16117435010755586603)
XLA Ops:
  0.0 18.4 %detect.1 = f32[4,8192]{1,0:T(4,128)S(1)} custom-call(s32[1,1024]{1,0:T(1,128)} %bitcast.1, s32[64,1024]{1,0:T(8,128)} %mask_hbm.1, f32[1024,1024]{1,0:T(8,128)} %traces_hbm.1, f32[4,8192]{1,0:T(4,128)} %template_hbm.1, bf16[144,384]{1,0:T(8,128)(2,1)} %constant.10.clone.first_hbm, bf16[768,256]{1,0:T(8,128)(2,1)} %constant.11.clone.forward_hbm, ...), custom_call_target="tpu_custom_call" | custom-call | tf_op jit(solution)/shard_map/detect/pallas_call | solution.py:447
  18.5 0.7 %copy.11 = f32[4,8192]{1,0:T(4,128)} copy(f32[4,8192]{1,0:T(4,128)S(1)} %detect.1) | data formatting | bytes 262144
